TPU v7x, 32 devices: a whole 2x2x4 slice. The times are simulated.
32 devices in a mesh: ctx: 8 (over z, x), fsdp: 4 (over y, core).
Axes of the slice: x: 2, y: 2, z: 4, core: 2. Of those that a mesh axis runs over, the one named last changes fastest.
Arguments:
- tokens: bfloat16 [4, 1024, 1600], P('fsdp', 'ctx'), may hold values from -40 to 40, as said below
- ln1_gain: bfloat16 [1600], P('fsdp'), may hold values from 0.099609375 to 1.8984375
- ln1_shift: bfloat16 [1600], P('fsdp'), may hold values from -3 to 3
- qkv_weight: bfloat16 [1600, 4800], P('fsdp'), may hold values from -0.15625 to 0.15625
- qv_bias: bfloat16 [3200], P('fsdp'), may hold values from -3 to 3
- out_weight: bfloat16 [1600, 1600], P('fsdp'), may hold values from -1.25 to 1.25
- out_bias: bfloat16 [1600], P('fsdp'), may hold values from -3 to 3
- ln2_gain: bfloat16 [1600], P('fsdp'), may hold values from 0.099609375 to 1.8984375
- ln2_shift: bfloat16 [1600], P('fsdp'), may hold values from -3 to 3
- up_weight: bfloat16 [1600, 6400], P('fsdp'), may hold values from -0.15625 to 0.15625
- up_bias: bfloat16 [6400], P('fsdp'), may hold values from -3 to 3
- down_weight: bfloat16 [6400, 1600], P('fsdp'), may hold values from -0.078125 to 0.078125
- down_bias: bfloat16 [1600], P('fsdp'), may hold values from -3 to 3
- block_table: int32 [8], replicated, may hold values from 0 to 7, each once
- cotangent: bfloat16 [4, 1024, 1600], P('fsdp', 'ctx'), may hold values from -6 to 6
Outputs:
- block_out: float32 [4, 1024, 1600], P('fsdp', 'ctx')
- input_grad: float32 [4, 1024, 1600], P('fsdp', 'ctx')
- ln1_gain_grad: float32 [1600], P('fsdp')
- ln1_shift_grad: float32 [1600], P('fsdp')
- qkv_weight_grad: float32 [1600, 4800], P('fsdp')
- qv_bias_grad: float32 [3200], P('fsdp')
- out_weight_grad: float32 [1600, 1600], P('fsdp')
- out_bias_grad: float32 [1600], P('fsdp')
- ln2_gain_grad: float32 [1600], P('fsdp')
- ln2_shift_grad: float32 [1600], P('fsdp')
- up_weight_grad: float32 [1600, 6400], P('fsdp')
- up_bias_grad: float32 [6400], P('fsdp')
- down_weight_grad: float32 [6400, 1600], P('fsdp')
- down_bias_grad: float32 [1600], P('fsdp')
Inputs may be any that keep to these rules, and one draw needn't show every extreme that they name: Device c of ctx holds blocks block_table[c] and 15 - block_table[c] of each of its sequence, in that order; every value appears once. `tokens`: activations of order one.
All inputs are finite; a program needn't handle non-finite values.
Results may differ from a plain program's by a relative error of at most 0.017.
Values may be sent and summed in bfloat16 or wider, within the bound.
A program may use at most 384 MiB of HBM per device.

v0:
```python
import jax
import jax.numpy as jnp
from jax import lax
from jax.sharding import PartitionSpec as P

HEAD_DIM = 64
EPS = 1e-05
SCALE = 0.125


def layer_norm(value, gain, shift):
    centre = value - jnp.mean(value, axis=-1, keepdims=True)
    spread = jnp.mean(centre * centre, axis=-1, keepdims=True)
    return centre * lax.rsqrt(spread + EPS) * gain + shift


def gelu_tanh(value):
    return jax.nn.gelu(value, approximate=True)


def inner_rows(left, right):
    return lax.dot_general(
        left, right, (((0,), (0,)), ((), ())), preferred_element_type=jnp.float32
    )


def times_transpose(left, right):
    return lax.dot_general(
        left, right, (((1,), (1,)), ((), ())), preferred_element_type=jnp.float32
    )


def exponents(query_part, query_place, key_part, key_place):
    raw = jnp.einsum("qhd,khd->hqk", query_part, key_part, preferred_element_type=jnp.float32)
    allowed = key_place[None, None, :] <= query_place[None, :, None]
    return jnp.where(allowed, jnp.exp(raw * SCALE), 0.0)


def score_grads(
    query_part, scaled_part, correction_part, query_place, key_part, value_part, key_place
):
    exponent = exponents(query_part, query_place, key_part, key_place)
    d_expo = jnp.einsum("qhd,khd->hqk", scaled_part, value_part, preferred_element_type=jnp.float32)
    d_raw = (exponent * (d_expo - correction_part.T[:, :, None])).astype(jnp.bfloat16) * SCALE
    return (exponent, d_raw)


def on_device(
    tokens,
    ln1_gain,
    ln1_shift,
    qkv_weight,
    qv_bias,
    out_weight,
    out_bias,
    ln2_gain,
    ln2_shift,
    up_weight,
    up_bias,
    down_weight,
    down_bias,
    block_table,
    cotangent,
):
    rows = tokens.shape[1]
    width = tokens.shape[2]
    heads = width // HEAD_DIM
    half = rows // 2
    count = lax.axis_size("ctx")
    within = jnp.arange(rows, dtype=jnp.int32)
    block_of = jnp.where(
        within[None, :] < half, block_table[:, None], 2 * count - 1 - block_table[:, None]
    )
    place = block_of * half + within[None, :] % half
    device = lax.axis_index("ctx")
    query_place = jnp.sum(
        jnp.where(jnp.arange(count, dtype=jnp.int32)[:, None] == device, place, 0), axis=0
    )
    key_place = place.reshape(-1)
    kblock = 4 * rows
    nblock = key_place.shape[0] // kblock
    place_blocks = key_place.reshape(nblock, kblock)
    attn_parts = (
        lax.all_gather(ln1_gain, "fsdp", axis=0, tiled=True),
        lax.all_gather(ln1_shift, "fsdp", axis=0, tiled=True),
        lax.all_gather(qkv_weight, "fsdp", axis=0, tiled=True),
        lax.all_gather(qv_bias, "fsdp", axis=0, tiled=True),
        lax.all_gather(out_weight, "fsdp", axis=0, tiled=True),
        lax.all_gather(out_bias, "fsdp", axis=0, tiled=True),
    )
    gain1 = attn_parts[0].astype(jnp.float32)
    shift1 = attn_parts[1].astype(jnp.float32)
    w_qkv = attn_parts[2]
    b_qv = attn_parts[3].astype(jnp.float32)
    w_out = attn_parts[4]
    b_out = attn_parts[5].astype(jnp.float32)
    inputs = tokens[0].astype(jnp.float32)
    normed1, ln1_back = jax.vjp(layer_norm, inputs, gain1, shift1)
    act1 = normed1.astype(jnp.bfloat16)
    projected = jnp.dot(act1, w_qkv, preferred_element_type=jnp.float32)
    query = (projected[:, :width] + b_qv[:width]).astype(jnp.bfloat16)
    keys = projected[:, width : 2 * width].astype(jnp.bfloat16)
    values = (projected[:, 2 * width :] + b_qv[width:]).astype(jnp.bfloat16)
    keys_all, values_all = (
        lax.all_gather(keys, "ctx", axis=0, tiled=True),
        lax.all_gather(values, "ctx", axis=0, tiled=True),
    )
    key_blocks = keys_all.reshape(nblock, kblock, heads, HEAD_DIM)
    value_blocks = values_all.reshape(nblock, kblock, heads, HEAD_DIM)
    query3 = query.reshape(rows, heads, HEAD_DIM)

    def forward_step(carry, parts):
        total, numerator = carry
        key_part, value_part, part_place = parts
        exponent = exponents(query3, query_place, key_part, part_place)
        total = total + jnp.sum(exponent, axis=2)
        numerator = numerator + jnp.einsum(
            "hqk,khd->qhd",
            exponent.astype(jnp.bfloat16),
            value_part,
            preferred_element_type=jnp.float32,
        )
        return ((total, numerator), None)

    begin = (jnp.zeros((heads, rows), jnp.float32), jnp.zeros((rows, heads, HEAD_DIM), jnp.float32))
    (total, numerator), _ = lax.scan(forward_step, begin, (key_blocks, value_blocks, place_blocks))
    totals_rows = total.T
    attended = numerator / totals_rows[:, :, None]
    attn = attended.reshape(rows, width).astype(jnp.bfloat16)
    mid = inputs + jnp.dot(attn, w_out, preferred_element_type=jnp.float32) + b_out
    mlp_parts = (
        lax.all_gather(ln2_gain, "fsdp", axis=0, tiled=True),
        lax.all_gather(ln2_shift, "fsdp", axis=0, tiled=True),
        lax.all_gather(up_weight, "fsdp", axis=0, tiled=True),
        lax.all_gather(up_bias, "fsdp", axis=0, tiled=True),
        lax.all_gather(down_weight, "fsdp", axis=0, tiled=True),
        lax.all_gather(down_bias, "fsdp", axis=0, tiled=True),
    )
    gain2 = mlp_parts[0].astype(jnp.float32)
    shift2 = mlp_parts[1].astype(jnp.float32)
    w_up = mlp_parts[2]
    b_up = mlp_parts[3].astype(jnp.float32)
    w_down = mlp_parts[4]
    b_down = mlp_parts[5].astype(jnp.float32)
    normed2, ln2_back = jax.vjp(layer_norm, mid, gain2, shift2)
    act2 = normed2.astype(jnp.bfloat16)
    hidden_in = jnp.dot(act2, w_up, preferred_element_type=jnp.float32) + b_up
    activated, gelu_back = jax.vjp(gelu_tanh, hidden_in)
    hidden = activated.astype(jnp.bfloat16)
    result = mid + jnp.dot(hidden, w_down, preferred_element_type=jnp.float32) + b_down
    grad_out = cotangent[0].astype(jnp.float32)
    grad_branch2 = grad_out.astype(jnp.bfloat16)
    d_down = inner_rows(hidden, grad_branch2)
    d_down_bias = jnp.sum(grad_branch2.astype(jnp.float32), axis=0)
    d_hidden = times_transpose(grad_branch2, w_down)
    d_hidden_in = gelu_back(d_hidden)[0].astype(jnp.bfloat16)
    d_up = inner_rows(act2, d_hidden_in)
    d_up_bias = jnp.sum(d_hidden_in.astype(jnp.float32), axis=0)
    d_act2 = times_transpose(d_hidden_in, w_up)
    d_mid_norm, d_gain2, d_shift2 = ln2_back(d_act2)
    mlp_owned = (
        lax.psum_scatter(d_gain2, "fsdp", scatter_dimension=0, tiled=True),
        lax.psum_scatter(d_shift2, "fsdp", scatter_dimension=0, tiled=True),
        lax.psum_scatter(d_up, "fsdp", scatter_dimension=0, tiled=True),
        lax.psum_scatter(d_up_bias, "fsdp", scatter_dimension=0, tiled=True),
        lax.psum_scatter(d_down, "fsdp", scatter_dimension=0, tiled=True),
        lax.psum_scatter(d_down_bias, "fsdp", scatter_dimension=0, tiled=True),
    )
    mlp_total = lax.psum(
        (mlp_owned[0], mlp_owned[1], mlp_owned[2], mlp_owned[3], mlp_owned[4], mlp_owned[5]), "ctx"
    )
    d_mid = grad_out + d_mid_norm
    grad_branch1 = d_mid.astype(jnp.bfloat16)
    d_out = inner_rows(attn, grad_branch1)
    d_out_bias = jnp.sum(grad_branch1.astype(jnp.float32), axis=0)
    d_attn = times_transpose(grad_branch1, w_out).reshape(rows, heads, HEAD_DIM)
    scaled = (d_attn / totals_rows[:, :, None]).astype(jnp.bfloat16)
    correction = jnp.sum(d_attn * attended, axis=2) / totals_rows
    zero_rows = jnp.zeros((rows, heads, HEAD_DIM), jnp.float32)

    def back_step(d_query, parts):
        key_part, value_part, part_place = parts
        exponent, d_raw = score_grads(
            query3, scaled, correction, query_place, key_part, value_part, part_place
        )
        d_query = d_query + jnp.einsum(
            "hqk,khd->qhd", d_raw, key_part, preferred_element_type=jnp.float32
        )
        d_key = jnp.einsum("hqk,qhd->khd", d_raw, query3, preferred_element_type=jnp.float32)
        d_value = jnp.einsum(
            "hqk,qhd->khd",
            exponent.astype(jnp.bfloat16),
            scaled,
            preferred_element_type=jnp.float32,
        )
        return (d_query, (d_key, d_value))

    d_query, (key_terms, value_terms) = lax.scan(
        back_step, zero_rows, (key_blocks, value_blocks, place_blocks)
    )
    d_keys, d_values = (
        lax.psum_scatter(key_terms.reshape(-1, width), "ctx", scatter_dimension=0, tiled=True),
        lax.psum_scatter(value_terms.reshape(-1, width), "ctx", scatter_dimension=0, tiled=True),
    )
    grad_query = d_query.reshape(rows, width).astype(jnp.bfloat16)
    grad_keys = d_keys.astype(jnp.bfloat16)
    grad_values = d_values.astype(jnp.bfloat16)
    grad_qkv = jnp.concatenate([grad_query, grad_keys, grad_values], axis=1)
    d_qkv = inner_rows(act1, grad_qkv)
    d_qv_bias = jnp.concatenate(
        [
            jnp.sum(grad_query.astype(jnp.float32), axis=0),
            jnp.sum(grad_values.astype(jnp.float32), axis=0),
        ]
    )
    d_act1 = times_transpose(grad_qkv, w_qkv)
    d_input_norm, d_gain1, d_shift1 = ln1_back(d_act1)
    input_grad = d_mid + d_input_norm
    attn_owned = (
        lax.psum_scatter(d_gain1, "fsdp", scatter_dimension=0, tiled=True),
        lax.psum_scatter(d_shift1, "fsdp", scatter_dimension=0, tiled=True),
        lax.psum_scatter(d_qkv, "fsdp", scatter_dimension=0, tiled=True),
        lax.psum_scatter(d_qv_bias, "fsdp", scatter_dimension=0, tiled=True),
        lax.psum_scatter(d_out, "fsdp", scatter_dimension=0, tiled=True),
        lax.psum_scatter(d_out_bias, "fsdp", scatter_dimension=0, tiled=True),
    )
    attn_total = lax.psum(
        (attn_owned[0], attn_owned[1], attn_owned[2], attn_owned[3], attn_owned[4], attn_owned[5]),
        "ctx",
    )
    return (
        result[None],
        input_grad[None],
        attn_total[0],
        attn_total[1],
        attn_total[2],
        attn_total[3],
        attn_total[4],
        attn_total[5],
        mlp_total[0],
        mlp_total[1],
        mlp_total[2],
        mlp_total[3],
        mlp_total[4],
        mlp_total[5],
    )


def solution(mesh):
    return jax.shard_map(
        on_device,
        mesh=mesh,
        in_specs=(
            P("fsdp", "ctx", None),
            P("fsdp"),
            P("fsdp"),
            P("fsdp", None),
            P("fsdp"),
            P("fsdp", None),
            P("fsdp"),
            P("fsdp"),
            P("fsdp"),
            P("fsdp", None),
            P("fsdp"),
            P("fsdp", None),
            P("fsdp"),
            P(),
            P("fsdp", "ctx", None),
        ),
        out_specs=(
            P("fsdp", "ctx", None),
            P("fsdp", "ctx", None),
            P("fsdp"),
            P("fsdp"),
            P("fsdp", None),
            P("fsdp"),
            P("fsdp", None),
            P("fsdp"),
            P("fsdp"),
            P("fsdp"),
            P("fsdp", None),
            P("fsdp"),
            P("fsdp", None),
            P("fsdp"),
        ),
        check_vma=False,
    )
```

profile of v0, /device:TPU:0, one launch (start us, length us, event | category | flops | bytes accessed | tf_op | source)
XLA Modules:
  0.0 3008.3 jit_solution(12149930245180257995)
XLA Ops:
  12.7 13.7 all-reduce.19
  27.1 84.4 %all-gather.7.cloned.1.call-done = bf16[1600,4800]{1,0:T(8,128)(2,1)} async-done(((bf16[400,4800]{1,0:T(8,128)(2,1)}), bf16[1600,4800]{1,0:T(8,128)(2,1)}) %all-gather.7.cloned.1.call-update) | async-done | bytes 15360016 | tf_op jit(solution)/shard_map/all_gather | solution.py:86
  111.4 10.6 fusion.98
  129.7 59.7 %all-gather.11.cloned.1.call-done = bf16[1024,1600]{0,1:T(8,128)(2,1)} async-done(((bf16[128,1600]{0,1:T(8,128)(2,1)}), bf16[1024,1600]{0,1:T(8,128)(2,1)}) %all-gather.11.cloned.1.call-update) | async-done | bytes 3276816 | tf_op jit(solution)/shard_map/all_gather | solution.py:106
  189.3 8.5 reshape.231
  197.8 4.4 copy.62
  202.3 52.1 %all-gather.9.cloned.1.call-done = bf16[1024,1600]{0,1:T(8,128)(2,1)} async-done(((bf16[128,1600]{0,1:T(8,128)(2,1)}), bf16[1024,1600]{0,1:T(8,128)(2,1)}) %all-gather.9.cloned.1.call-update) | async-done | bytes 3276816 | tf_op jit(solution)/shard_map/all_gather | solution.py:105
  254.3 8.5 reshape.229
  262.9 4.9 copy.61
  267.8 12.9 while.28
  280.8 14.0 all-gather.13.cloned.1.call-done
  294.8 4.8 fusion.106
  299.9 125.3 %all-gather.15.cloned.1.call-done = bf16[1600,6400]{1,0:T(8,128)(2,1)} async-done(((bf16[400,6400]{1,0:T(8,128)(2,1)}), bf16[1600,6400]{1,0:T(8,128)(2,1)}) %all-gather.15.cloned.1.call-update) | async-done | bytes 20480016 | tf_op jit(solution)/shard_map/all_gather | solution.py:134
  425.2 12.2 convolution_add_fusion
  437.4 122.6 %all-gather.17.cloned.1.call-done = bf16[6400,1600]{1,0:T(8,128)(2,1)} async-done(((bf16[1600,1600]{1,0:T(8,128)(2,1)}), bf16[6400,1600]{1,0:T(8,128)(2,1)}) %all-gather.17.cloned.1.call-update) | async-done | bytes 20480016 | tf_op jit(solution)/shard_map/all_gather | solution.py:136
  560.0 11.9 convert_reduce_fusion
  572.0 12.7 multiply_reduce_fusion
  588.6 281.8 %while.29 = (s32[]{:T(128)}, f32[128,25,64]{0,2,1:T(8,128)}, f32[2,512,25,64]{1,0,3,2:T(2,128)}, f32[2,512,25,64]{1,0,3,2:T(2,128)}, bf16[2,512,25,64]{1,3,2,0:T...) while((s32[]{:T(128)}, f32[128,25,64]{0,2,1:T(8,128)}, ...), condition=%wide.region_12.13_spmd.clone, body=%wide.region_11.12_spmd.clone.sunk | while | flops 1063796736 | bytes 77221088 | solution.py:198
  591.7 4.0 fusion.165
  598.1 3.4 copy.102
  606.7 5.1 copy.101
  611.8 59.0 %dynamic_update_slice.11 = f32[2,512,25,64]{1,0,3,2:T(2,128)} dynamic-update-slice(f32[2,512,25,64]{1,0,3,2:T(2,128)} %get-tuple-element.526, f32[1,512,25,64]{1,0,3,2:T(1,128)} %copy.101, s32[]{:T(128)S(6)} %copy.126, s32[]{:T(128)} %constant.73.clone.1..sunk.1, s32[]{:T(128)} %constant.73.clone.1..sunk.1, s32[]{:T(128)} %constant.73.clone.1..sunk.1) | dynamic-update-slice | bytes 6553604 | tf_op jit(solution)/shard_map/while/body/jit(dynamic_update_index_in_dim)/dynamic_update_slice | solution.py:198
  670.8 58.8 %dynamic_update_slice.12 = f32[2,512,25,64]{1,0,3,2:T(2,128)} dynamic-update-slice(f32[2,512,25,64]{1,0,3,2:T(2,128)} %get-tuple-element.527, f32[1,512,25,64]{1,0,3,2:T(1,128)S(1)} %copy.102, s32[]{:T(128)S(6)} %copy.126, s32[]{:T(128)} %constant.73.clone.1..sunk.1, s32[]{:T(128)} %constant.73.clone.1..sunk.1, s32[]{:T(128)} %constant.73.clone.1..sunk.1) | dynamic-update-slice | bytes 6553604 | tf_op jit(solution)/shard_map/while/body/jit(dynamic_update_index_in_dim)/dynamic_update_slice | solution.py:198
  732.3 4.0 fusion.165
  738.7 3.4 copy.102
  747.3 5.1 copy.101
  752.4 59.0 %dynamic_update_slice.11 = f32[2,512,25,64]{1,0,3,2:T(2,128)} dynamic-update-slice(f32[2,512,25,64]{1,0,3,2:T(2,128)} %get-tuple-element.526, f32[1,512,25,64]{1,0,3,2:T(1,128)} %copy.101, s32[]{:T(128)S(6)} %copy.126, s32[]{:T(128)} %constant.73.clone.1..sunk.1, s32[]{:T(128)} %constant.73.clone.1..sunk.1, s32[]{:T(128)} %constant.73.clone.1..sunk.1) | dynamic-update-slice | bytes 6553604 | tf_op jit(solution)/shard_map/while/body/jit(dynamic_update_index_in_dim)/dynamic_update_slice | solution.py:198
  811.4 58.8 %dynamic_update_slice.12 = f32[2,512,25,64]{1,0,3,2:T(2,128)} dynamic-update-slice(f32[2,512,25,64]{1,0,3,2:T(2,128)} %get-tuple-element.527, f32[1,512,25,64]{1,0,3,2:T(1,128)S(1)} %copy.102, s32[]{:T(128)S(6)} %copy.126, s32[]{:T(128)} %constant.73.clone.1..sunk.1, s32[]{:T(128)} %constant.73.clone.1..sunk.1, s32[]{:T(128)} %constant.73.clone.1..sunk.1) | dynamic-update-slice | bytes 6553604 | tf_op jit(solution)/shard_map/while/body/jit(dynamic_update_index_in_dim)/dynamic_update_slice | solution.py:198
  870.4 7.2 copy.95
  877.7 7.3 copy.96
  886.1 5.7 fusion.107
  893.2 106.7 %reduce-scatter.7.cloned.1.call-done = f32[128,1600]{0,1:T(8,128)} async-done(((f32[1024,1600]{0,1:T(8,128)}), f32[128,1600]{0,1:T(8,128)}) %reduce-scatter.7.cloned.1.call-update) | async-done | bytes 819216 | tf_op jit(solution)/shard_map/reduce_scatter | solution.py:202
  1001.1 124.4 %reduce-scatter.9.cloned.1.call-done = f32[128,1600]{0,1:T(8,128)} async-done(((f32[1024,1600]{0,1:T(8,128)}), f32[128,1600]{0,1:T(8,128)}) %reduce-scatter.9.cloned.1.call-update) | async-done | bytes 819216 | tf_op jit(solution)/shard_map/reduce_scatter | solution.py:203
  1127.0 17.7 fusion.81
  1146.5 17.3 fusion.100
  1164.7 18.8 fusion.83
  1184.7 9.8 fusion.101
  1197.7 15.6 reduce-scatter.13.cloned.1.call-done
  1213.4 224.2 %reduce-scatter.11.cloned.1.call-done = f32[400,4800]{1,0:T(8,128)} async-done(((f32[1600,4800]{1,0:T(8,128)}), f32[400,4800]{1,0:T(8,128)}) %reduce-scatter.11.cloned.1.call-update) | async-done | bytes 7680016 | tf_op jit(solution)/shard_map/reduce_scatter | solution.py:222
  1437.5 295.6 %reduce-scatter.15.cloned.1.call-done = f32[400,6400]{1,0:T(8,128)} async-done(((f32[1600,6400]{1,0:T(8,128)}), f32[400,6400]{1,0:T(8,128)}) %reduce-scatter.15.cloned.1.call-update) | async-done | bytes 10240016 | tf_op jit(solution)/shard_map/reduce_scatter | solution.py:164
  1733.2 289.2 %reduce-scatter.17.cloned.1.call-done = f32[1600,1600]{1,0:T(8,128)} async-done(((f32[6400,1600]{1,0:T(8,128)}), f32[1600,1600]{1,0:T(8,128)}) %reduce-scatter.17.cloned.1.call-update) | async-done | bytes 10240016 | tf_op jit(solution)/shard_map/reduce_scatter | solution.py:166
  2024.3 14.6 fusion.65
  2038.9 19.7 all-reduce.25.cloned.1.call-done
  2064.9 39.9 %all-reduce.16 = (f32[400]{0:T(512)}, f32[400]{0:T(512)}, f32[800]{0:T(1024)}, f32[400]{0:T(512)}, f32[400]{0:T(512)}, /*index=5*/f32[400]{0:T(512)}, f32[1600]{0:T(1024)}, f32[400]{0:T(512)}) all-reduce(f32[400]{0:T(512)S(1)} %dynamic-slice.9, f32[400]{0:T(512)S(1)} %dynamic-slice.11, ...), channel_id=1, replica_groups=mesh['ctx'=8,'fsdp'=4] {'ctx'}, use_global_device_ids=true, to_apply=%region_19.20 | all-reduce | flops 4800 | bytes 38400 | tf_op jit(solution)/shard_map/psum | solution.py:227
  2104.8 874.7 %all-reduce.23.cloned.1.call-done = (f32[400,4800]{1,0:T(8,128)}, f32[400,1600]{1,0:T(8,128)}, f32[400,6400]{1,0:T(8,128)}, f32[1600,1600]{1,0:T(8,128)}) async-done(((f32[400,4800]{1,0:T(8,128)}, f32[400,1600]{1,0:T(8,128)}, f32[400,6400]{1,0:T(8,128)}, f32[1600,1600]{1,0:T(8,128)}), (f32[400,4800]{1,0:T(8,128)}, f32[400,1600]{1,0:T(8,128)}, f32[400,6400]{1,0:T(8,128)}, ...) | async-done | bytes 30720016 | tf_op jit(solution)/shard_map/psum | solution.py:227
  2979.5 7.1 copy.146
  2988.1 9.3 copy.148
  2997.4 4.1 copy.149
  (238 shorter events, 68.7 us)
Async XLA Ops:
  7.2 3.7 copy-start.40
  7.2 3.9 copy-start.41
  7.2 4.2 copy-start.42
  7.2 4.4 copy-start.43
  7.2 4.7 copy-start.44
  7.3 4.9 copy-start.38
  7.3 5.2 copy-start.34
  7.3 19.2 copy-start.5
  7.3 104.1 %all-gather.7.cloned.1.call-start = ((), (), s32[]{:S(2)}) async-start(), calls=%async_computation.6 | async-start | bytes 19456000 | tf_op jit(solution)/shard_map/all_gather | solution.py:86
  8.0 181.3 %all-gather.11.cloned.1.call-start = ((), (), s32[]{:S(2)}) async-start(), calls=%async_computation.8 | async-start | bytes 3686400 | tf_op jit(solution)/shard_map/all_gather | solution.py:106
  26.5 95.6 %copy-start.25 = (f32[1600]{0:T(1024)}, f32[1600]{0:T(1024)S(1)}, u32[]{:S(2)}) copy-start(f32[1600]{0:T(1024)S(1)} %convert_element_type.104) | copy-start | bytes 19204
  26.5 95.6 %copy-start.23 = (f32[1600]{0:T(1024)}, f32[1600]{0:T(1024)S(1)}, u32[]{:S(2)}) copy-start(f32[1600]{0:T(1024)S(1)} %convert_element_type.103) | copy-start | bytes 19204
  26.7 95.3 %copy-start.29 = (f32[128]{0:T(128)}, f32[128]{0:T(128)S(1)}, u32[]{:S(2)}) copy-start(f32[128]{0:T(128)S(1)} %broadcast_multiply_fusion.1) | copy-start | bytes 1540
  27.0 95.1 %copy-start.45 = (f32[128]{0:T(128)}, f32[128]{0:T(128)S(1)}, u32[]{:S(2)}) copy-start(f32[128]{0:T(128)S(1)} %fusion.76) | copy-start | bytes 1540
  27.0 95.1 %copy-start.31 = (f32[128]{0:T(128)}, f32[128]{0:T(128)S(1)}, u32[]{:S(2)}) copy-start(f32[128]{0:T(128)S(1)} %fusion.93) | copy-start | bytes 1540
  124.9 129.4 %all-gather.9.cloned.1.call-start = ((), (), s32[]{:S(2)}) async-start(), calls=%async_computation.7 | async-start | bytes 3686400 | tf_op jit(solution)/shard_map/all_gather | solution.py:105
  126.9 167.9 %all-gather.13.cloned.1.call-start = ((), (), s32[]{:S(2)}) async-start(), calls=%async_computation.9 | async-start | bytes 6656000 | tf_op jit(solution)/shard_map/all_gather | solution.py:88
  127.5 297.6 %all-gather.15.cloned.1.call-start = ((), (), s32[]{:S(2)}) async-start(), calls=%async_computation.10 | async-start | bytes 25600000 | tf_op jit(solution)/shard_map/all_gather | solution.py:134
  128.1 431.9 %all-gather.17.cloned.1.call-start = ((), (), s32[]{:S(2)}) async-start(), calls=%async_computation.11 | async-start | bytes 26624000 | tf_op jit(solution)/shard_map/all_gather | solution.py:136
  128.7 871.2 %reduce-scatter.7.cloned.1.call-start = ((), (), s32[]{:S(2)}) async-start(), calls=%async_computation.12 | async-start | bytes 7372800 | tf_op jit(solution)/shard_map/reduce_scatter | solution.py:202
  129.4 295.7 %copy-start.27 = (f32[1600]{0:T(1024)}, f32[1600]{0:T(1024)S(1)}, u32[]{:S(2)}) copy-start(f32[1600]{0:T(1024)S(1)} %convert_element_type.113) | copy-start | bytes 19204
  280.8 18.8 copy-start.12
  299.6 285.1 %copy-start = (f32[128,1600]{0,1:T(8,128)}, f32[128,1600]{0,1:T(8,128)S(1)}, u32[]{:S(2)}) copy-start(f32[128,1600]{0,1:T(8,128)S(1)} %get-tuple-element.354) | copy-start | bytes 2457604
  299.9 260.2 %copy-start.14 = (bf16[1,128,1600]{1,2,0:T(8,128)(2,1)S(1)}, bf16[1,128,1600]{1,2,0:T(8,128)(2,1)}, u32[]{:S(2)}) copy-start(bf16[1,128,1600]{1,2,0:T(8,128)(2,1)} %param.33) | copy-start | bytes 1228804
  572.0 12.7 copy-start.7
  572.0 14.0 slice-start
  572.0 14.0 slice-start.1
  877.6 247.9 %reduce-scatter.9.cloned.1.call-start = ((), (), s32[]{:S(2)}) async-start(), calls=%async_computation.13 | async-start | bytes 7372800 | tf_op jit(solution)/shard_map/reduce_scatter | solution.py:203
  885.0 328.4 %reduce-scatter.13.cloned.1.call-start = ((), (), s32[]{:S(2)}) async-start(), calls=%async_computation.15 | async-start | bytes 13312000 | tf_op jit(solution)/shard_map/reduce_scatter | solution.py:224
  891.8 235.1 %copy-start.6 = (bf16[1,128,1600]{1,2,0:T(8,128)(2,1)S(1)}, bf16[1,128,1600]{1,2,0:T(8,128)(2,1)}, u32[]{:S(2)}) copy-start(bf16[1,128,1600]{1,2,0:T(8,128)(2,1)} %param.19) | copy-start | bytes 1228804
  891.8 235.1 %copy-start.24 = (f32[1600]{0:T(1024)S(1)}, f32[1600]{0:T(1024)}, u32[]{:S(2)}) copy-start(f32[1600]{0:T(1024)} %copy-done.23) | copy-start | bytes 19204
  891.8 235.1 %copy-start.26 = (f32[1600]{0:T(1024)S(1)}, f32[1600]{0:T(1024)}, u32[]{:S(2)}) copy-start(f32[1600]{0:T(1024)} %copy-done.25) | copy-start | bytes 19204
  891.8 235.1 %copy-start.30 = (f32[128]{0:T(128)S(1)}, f32[128]{0:T(128)}, u32[]{:S(2)}) copy-start(f32[128]{0:T(128)} %copy-done.29) | copy-start | bytes 1540
  891.9 235.1 %copy-start.32 = (f32[128]{0:T(128)S(1)}, f32[128]{0:T(128)}, u32[]{:S(2)}) copy-start(f32[128]{0:T(128)} %copy-done.31) | copy-start | bytes 1540
  891.9 545.7 %reduce-scatter.11.cloned.1.call-start = ((), (), s32[]{:S(2)}) async-start(), calls=%async_computation.14 | async-start | bytes 38912000 | tf_op jit(solution)/shard_map/reduce_scatter | solution.py:222
  1001.1 143.6 %copy-start.19 = (bf16[128,1600]{0,1:T(8,128)(2,1)}, bf16[128,1600]{0,1:T(8,128)(2,1)S(1)}, u32[]{:S(2)}) copy-start(bf16[128,1600]{0,1:T(8,128)(2,1)S(1)} %convert_element_type.124) | copy-start | bytes 1228804
  1126.9 17.7 copy-start.21
  1144.7 588.4 %reduce-scatter.15.cloned.1.call-start = ((), (), s32[]{:S(2)}) async-start(), calls=%async_computation.16 | async-start | bytes 51200000 | tf_op jit(solution)/shard_map/reduce_scatter | solution.py:164
  1163.8 858.6 %reduce-scatter.17.cloned.1.call-start = ((), (), s32[]{:S(2)}) async-start(), calls=%async_computation.17 | async-start | bytes 53248000 | tf_op jit(solution)/shard_map/reduce_scatter | solution.py:166
  1183.6 875.1 %all-reduce.25.cloned.1.call-start = ((), (), s32[]{:S(2)}) async-start(), calls=%async_computation.19 | async-start | bytes 188416
  1184.7 9.8 copy-start.46
  1184.7 11.0 copy-start.11
  1184.7 11.0 copy-start.36
  1197.7 1781.8 %all-reduce.23.cloned.1.call-start = ((), (), s32[]{:S(2)}) async-start(), calls=%async_computation.18 | async-start | bytes 62668800 | tf_op jit(solution)/shard_map/psum | solution.py:227
  2979.5 7.1 copy-start.18
  2986.5 10.8 slice-start.2
  2988.1 9.3 slice-start.3
  2988.1 9.3 slice-start.4
  (21 other events, 38.7 us)
Sparse Core Ops, SparseCore 0:
  9.7 101.7 all-gather.6
  125.0 64.2 all-gather.10
  192.0 62.3 all-gather.8
  255.7 39.0 all-gather.12
  296.3 128.8 all-gather.14
  426.6 133.3 all-gather.16
  877.7 122.1 reduce-scatter.6
  1004.1 121.3 reduce-scatter.8
  1128.7 84.6 reduce-scatter.12
  1215.9 221.6 reduce-scatter.10
  1440.2 292.9 reduce-scatter.14
  1735.6 286.6 reduce-scatter.16
  2026.3 32.3 all-reduce.24
  2063.4 916.0 all-reduce.22
where the time goes:
time: 3030 us; the launch traced here: 3010 us
  waiting for transfers between devices  2410 us (80%)
  local copies, waits for them, and re-layouts  333 us (11%)
  matrix products  178 us (6%)
  blocking collectives  53.7 us (2%)
    psum x1, waiting for transfers between devices, on_device(): lax.psum((attn_owned[0], attn_owned[1], attn_owned[2], attn_owned[3], att...  875 us
    reduce_scatter x1, waiting for transfers between devices, on_device(): lax.psum_scatter(d_up, 'fsdp', scatter_dimension=0, tiled=True)  296 us
    reduce_scatter x1, waiting for transfers between devices, on_device(): lax.psum_scatter(d_down, 'fsdp', scatter_dimension=0, tiled=True)  289 us
    dynamic_update_slice x8, local copies, waits for them, and re-layouts, on_device(): lax.scan(back_step, zero_rows, (key_blocks, value_blocks, place_blocks))  253 us
    reduce_scatter x1, waiting for transfers between devices, on_device(): lax.psum_scatter(d_qkv, 'fsdp', scatter_dimension=0, tiled=True)  224 us
    all_gather x1, waiting for transfers between devices, on_device(): lax.all_gather(up_weight, 'fsdp', axis=0, tiled=True)  125 us
    reduce_scatter x1, waiting for transfers between devices, on_device(): lax.psum_scatter(value_terms.reshape(-1, width), 'ctx', scatter_dimension...  124 us
    all_gather x1, waiting for transfers between devices, on_device(): lax.all_gather(down_weight, 'fsdp', axis=0, tiled=True)  123 us
  transfers between devices with their start and end apart: 14, of which 14 were waited for; matrix products, arithmetic and copies ran while one was open for 6% of the time, Pallas kernels for 0%

commit v1 on v0

--- a/solution.py
+++ b/solution.py
@@ -80,10 +80,24 @@
     kblock = 4 * rows
     nblock = key_place.shape[0] // kblock
     place_blocks = key_place.reshape(nblock, kblock)
+
+    def draw_tiles(vec):
+        ax_name = "fsdp"
+        p_count = jax.lax.axis_size(ax_name)
+        samples = [vec]
+        for d in [*range(1, p_count)]:
+            moved = jax.lax.ppermute(
+                samples[d - 1], ax_name, [(kk, (kk - 1) % p_count) for kk in range(p_count)]
+            )
+            samples.append(moved)
+        current_arr = jnp.concatenate(samples, 0)
+        next_value = jax.lax.axis_index(ax_name)
+        return jnp.roll(current_arr, next_value * vec.shape[0], axis=0)
+
     attn_parts = (
         lax.all_gather(ln1_gain, "fsdp", axis=0, tiled=True),
         lax.all_gather(ln1_shift, "fsdp", axis=0, tiled=True),
-        lax.all_gather(qkv_weight, "fsdp", axis=0, tiled=True),
+        draw_tiles(qkv_weight),
         lax.all_gather(qv_bias, "fsdp", axis=0, tiled=True),
         lax.all_gather(out_weight, "fsdp", axis=0, tiled=True),
         lax.all_gather(out_bias, "fsdp", axis=0, tiled=True),

time: 3030 us -> 3110 us (1.026)
  local copies, waits for them, and re-layouts: 333 us -> 365 us
    ppermute x0 -> x3, waiting for transfers between devices: none -> 85.9 us  [draw_tiles(): jax.lax.ppermute(samples[d - 1], ax_name, [(kk, (kk - 1) % p_count) for k...]
    all_gather x1 -> x0, waiting for transfers between devices: 84.4 us -> none  [on_device(): lax.all_gather(qkv_weight, 'fsdp', axis=0, tiled=True)]
    unnamed x136 -> x131, local copies, waits for them, and re-layouts: 61.4 us -> 93.2 us
  transfers between devices with their start and end apart: 14 -> 16, of which waited for: 14 -> 15; matrix products, arithmetic and copies ran while one was open for 6% -> 6% of each run, Pallas kernels for 0% -> 0%
where the time goes in v1:
time: 3110 us; the launch traced here: 3080 us
  waiting for transfers between devices  2400 us (77%)
  local copies, waits for them, and re-layouts  365 us (12%)
  matrix products  195 us (6%)
  blocking collectives  81.4 us (3%)
    psum x1, waiting for transfers between devices, on_device(): lax.psum((attn_owned[0], attn_owned[1], attn_owned[2], attn_owned[3], att...  875 us
    reduce_scatter x1, waiting for transfers between devices, on_device(): lax.psum_scatter(d_up, 'fsdp', scatter_dimension=0, tiled=True)  295 us
    reduce_scatter x1, waiting for transfers between devices, on_device(): lax.psum_scatter(d_down, 'fsdp', scatter_dimension=0, tiled=True)  289 us
    dynamic_update_slice x8, local copies, waits for them, and re-layouts, on_device(): lax.scan(back_step, zero_rows, (key_blocks, value_blocks, place_blocks))  249 us
    reduce_scatter x1, waiting for transfers between devices, on_device(): lax.psum_scatter(d_qkv, 'fsdp', scatter_dimension=0, tiled=True)  224 us
    all_gather x1, waiting for transfers between devices, on_device(): lax.all_gather(up_weight, 'fsdp', axis=0, tiled=True)  125 us
    reduce_scatter x1, waiting for transfers between devices, on_device(): lax.psum_scatter(value_terms.reshape(-1, width), 'ctx', scatter_dimension...  124 us
    all_gather x1, waiting for transfers between devices, on_device(): lax.all_gather(down_weight, 'fsdp', axis=0, tiled=True)  123 us
  transfers between devices with their start and end apart: 16, of which 15 were waited for; matrix products, arithmetic and copies ran while one was open for 6% of the time, Pallas kernels for 0%

profile of v1, /device:TPU:0, one launch (start us, length us, event | category | flops | bytes accessed | tf_op | source)
XLA Modules:
  0.0 3083.4 jit_solution(2622517077100259733)
XLA Ops:
  9.7 43.1 %collective-permute-done = bf16[400,4800]{1,0:T(8,128)(2,1)S(1)} collective-permute-done((bf16[400,4800]{1,0:T(8,128)(2,1)}, bf16[400,4800]{1,0:T(8,128)(2,1)S(1)}, u32[]{:S(2)}, u32[]{:S(2)}) %collective-permute-start) | collective-permute-done | bytes 3840032 | tf_op jit(solution)/shard_map/ppermute | solution.py:89
  56.5 42.8 %collective-permute-done.1 = bf16[400,4800]{1,0:T(8,128)(2,1)} collective-permute-done((bf16[400,4800]{1,0:T(8,128)(2,1)S(1)}, bf16[400,4800]{1,0:T(8,128)(2,1)}, u32[]{:S(2)}, u32[]{:S(2)}) %collective-permute-start.1) | collective-permute-done | bytes 3840032 | tf_op jit(solution)/shard_map/ppermute | solution.py:89
  111.6 41.3 %all-reduce.19 = (bf16[1600]{0:T(1024)(128)(2,1)S(1)}, bf16[1600]{0:T(1024)(128)(2,1)S(1)}, bf16[3200]{0:T(1024)(128)(2,1)S(1)}, bf16[1600]{0:T(1024)(128)(2,1)S...) all-reduce(bf16[1600]{0:T(1024)(128)(2,1)S(1)} %dynamic-update-slic, ...), channel_id=1, replica_groups=mesh['ctx'=8,'fsdp'=4] {'fsdp'}, use_global_device_ids=true, to_apply=%add.1 | all-reduce | flops 19200 | bytes 76800
  183.4 11.3 fusion.58
  202.8 58.8 %all-gather.6.cloned.1.call-done = bf16[1024,1600]{0,1:T(8,128)(2,1)} async-done(((bf16[128,1600]{0,1:T(8,128)(2,1)}), bf16[1024,1600]{0,1:T(8,128)(2,1)}) %all-gather.6.cloned.1.call-update) | async-done | bytes 3276816 | tf_op jit(solution)/shard_map/all_gather | solution.py:119
  261.6 8.5 reshape.229
  270.1 4.4 copy.61
  274.5 51.5 %all-gather.8.cloned.1.call-done = bf16[1024,1600]{0,1:T(8,128)(2,1)} async-done(((bf16[128,1600]{0,1:T(8,128)(2,1)}), bf16[1024,1600]{0,1:T(8,128)(2,1)}) %all-gather.8.cloned.1.call-update) | async-done | bytes 3276816 | tf_op jit(solution)/shard_map/all_gather | solution.py:120
  326.0 8.5 reshape.231
  334.6 5.0 copy.62
  339.6 22.3 while.28
  339.7 6.0 fusion.154
  345.8 4.8 fusion.155
  350.8 6.0 fusion.154
  356.9 4.8 fusion.155
  362.0 4.7 all-gather.10.cloned.1.call-done
  366.7 4.8 fusion.110
  371.7 125.3 %all-gather.12.cloned.1.call-done = bf16[1600,6400]{1,0:T(8,128)(2,1)} async-done(((bf16[400,6400]{1,0:T(8,128)(2,1)}), bf16[1600,6400]{1,0:T(8,128)(2,1)}) %all-gather.12.cloned.1.call-update) | async-done | bytes 20480016 | tf_op jit(solution)/shard_map/all_gather | solution.py:148
  497.0 12.2 convolution_add_fusion
  509.3 122.6 %all-gather.14.cloned.1.call-done = bf16[6400,1600]{1,0:T(8,128)(2,1)} async-done(((bf16[1600,1600]{1,0:T(8,128)(2,1)}), bf16[6400,1600]{1,0:T(8,128)(2,1)}) %all-gather.14.cloned.1.call-update) | async-done | bytes 20480016 | tf_op jit(solution)/shard_map/all_gather | solution.py:150
  631.9 12.1 convert_reduce_fusion
  644.0 12.7 multiply_reduce_fusion
  660.6 284.8 %while.29 = (s32[]{:T(128)}, f32[128,25,64]{0,2,1:T(8,128)}, f32[2,512,25,64]{1,0,3,2:T(2,128)}, f32[2,512,25,64]{1,0,3,2:T(2,128)}, bf16[2,512,25,64]{1,3,2,0:T...) while((s32[]{:T(128)}, f32[128,25,64]{0,2,1:T(8,128)}, ...), condition=%wide.region_12.13_spmd.clone, body=%wide.region_11.12_spmd.clone.sunk | while | flops 1063796736 | bytes 98520288 | solution.py:212
  663.8 5.2 fusion.167
  677.8 58.8 %dynamic_update_slice.11 = f32[2,512,25,64]{1,0,3,2:T(2,128)} dynamic-update-slice(f32[2,512,25,64]{1,0,3,2:T(2,128)} %get-tuple-element.526, f32[1,512,25,64]{1,0,3,2:T(1,128)S(1)} %copy.101, s32[]{:T(128)S(6)} %copy.133, s32[]{:T(128)} %constant.92.clone.1..sunk.1, s32[]{:T(128)} %constant.92.clone.1..sunk.1, s32[]{:T(128)} %constant.92.clone.1..sunk.1) | dynamic-update-slice | bytes 6553604 | tf_op jit(solution)/shard_map/while/body/jit(dynamic_update_index_in_dim)/dynamic_update_slice | solution.py:212
  744.2 58.8 %dynamic_update_slice.12 = f32[2,512,25,64]{1,0,3,2:T(2,128)} dynamic-update-slice(f32[2,512,25,64]{1,0,3,2:T(2,128)} %get-tuple-element.527, f32[1,512,25,64]{1,0,3,2:T(1,128)S(1)} %copy.102, s32[]{:T(128)S(6)} %copy.133, s32[]{:T(128)} %constant.92.clone.1..sunk.1, s32[]{:T(128)} %constant.92.clone.1..sunk.1, s32[]{:T(128)} %constant.92.clone.1..sunk.1) | dynamic-update-slice | bytes 6553604 | tf_op jit(solution)/shard_map/while/body/jit(dynamic_update_index_in_dim)/dynamic_update_slice | solution.py:212
  805.8 5.2 fusion.167
  820.0 58.8 %dynamic_update_slice.11 = f32[2,512,25,64]{1,0,3,2:T(2,128)} dynamic-update-slice(f32[2,512,25,64]{1,0,3,2:T(2,128)} %get-tuple-element.526, f32[1,512,25,64]{1,0,3,2:T(1,128)S(1)} %copy.101, s32[]{:T(128)S(6)} %copy.133, s32[]{:T(128)} %constant.92.clone.1..sunk.1, s32[]{:T(128)} %constant.92.clone.1..sunk.1, s32[]{:T(128)} %constant.92.clone.1..sunk.1) | dynamic-update-slice | bytes 6553604 | tf_op jit(solution)/shard_map/while/body/jit(dynamic_update_index_in_dim)/dynamic_update_slice | solution.py:212
  886.4 58.8 %dynamic_update_slice.12 = f32[2,512,25,64]{1,0,3,2:T(2,128)} dynamic-update-slice(f32[2,512,25,64]{1,0,3,2:T(2,128)} %get-tuple-element.527, f32[1,512,25,64]{1,0,3,2:T(1,128)S(1)} %copy.102, s32[]{:T(128)S(6)} %copy.133, s32[]{:T(128)} %constant.92.clone.1..sunk.1, s32[]{:T(128)} %constant.92.clone.1..sunk.1, s32[]{:T(128)} %constant.92.clone.1..sunk.1) | dynamic-update-slice | bytes 6553604 | tf_op jit(solution)/shard_map/while/body/jit(dynamic_update_index_in_dim)/dynamic_update_slice | solution.py:212
  945.4 7.2 copy.95
  952.7 7.3 copy.96
  961.1 5.7 fusion.111
  968.3 106.7 %reduce-scatter.7.cloned.1.call-done = f32[128,1600]{0,1:T(8,128)} async-done(((f32[1024,1600]{0,1:T(8,128)}), f32[128,1600]{0,1:T(8,128)}) %reduce-scatter.7.cloned.1.call-update) | async-done | bytes 819216 | tf_op jit(solution)/shard_map/reduce_scatter | solution.py:216
  1076.2 124.4 %reduce-scatter.9.cloned.1.call-done = f32[128,1600]{0,1:T(8,128)} async-done(((f32[1024,1600]{0,1:T(8,128)}), f32[128,1600]{0,1:T(8,128)}) %reduce-scatter.9.cloned.1.call-update) | async-done | bytes 819216 | tf_op jit(solution)/shard_map/reduce_scatter | solution.py:217
  1202.1 17.7 fusion.85
  1221.5 17.3 fusion.104
  1239.8 18.8 fusion.86
  1259.8 9.9 fusion.105
  1272.9 15.6 reduce-scatter.13.cloned.1.call-done
  1288.5 224.3 %reduce-scatter.11.cloned.1.call-done = f32[400,4800]{1,0:T(8,128)} async-done(((f32[1600,4800]{1,0:T(8,128)}), f32[400,4800]{1,0:T(8,128)}) %reduce-scatter.11.cloned.1.call-update) | async-done | bytes 7680016 | tf_op jit(solution)/shard_map/reduce_scatter | solution.py:236
  1512.8 295.5 %reduce-scatter.15.cloned.1.call-done = f32[400,6400]{1,0:T(8,128)} async-done(((f32[1600,6400]{1,0:T(8,128)}), f32[400,6400]{1,0:T(8,128)}) %reduce-scatter.15.cloned.1.call-update) | async-done | bytes 10240016 | tf_op jit(solution)/shard_map/reduce_scatter | solution.py:178
  1808.3 289.3 %reduce-scatter.17.cloned.1.call-done = f32[1600,1600]{1,0:T(8,128)} async-done(((f32[6400,1600]{1,0:T(8,128)}), f32[1600,1600]{1,0:T(8,128)}) %reduce-scatter.17.cloned.1.call-update) | async-done | bytes 10240016 | tf_op jit(solution)/shard_map/reduce_scatter | solution.py:180
  2100.2 14.6 fusion.69
  2114.8 18.9 all-reduce.25.cloned.1.call-done
  2139.9 40.1 %all-reduce.16 = (f32[400]{0:T(512)}, f32[400]{0:T(512)}, f32[800]{0:T(1024)}, f32[400]{0:T(512)}, f32[400]{0:T(512)}, /*index=5*/f32[400]{0:T(512)}, f32[1600]{0:T(1024)}, f32[400]{0:T(512)}) all-reduce(f32[400]{0:T(512)S(1)} %dynamic-slice.9, f32[400]{0:T(512)S(1)} %dynamic-slice.11, ...), channel_id=1, replica_groups=mesh['ctx'=8,'fsdp'=4] {'ctx'}, use_global_device_ids=true, to_apply=%region_19.20 | all-reduce | flops 4800 | bytes 38400 | tf_op jit(solution)/shard_map/psum | solution.py:241
  2180.0 874.7 %all-reduce.23.cloned.1.call-done = (f32[400,4800]{1,0:T(8,128)}, f32[400,1600]{1,0:T(8,128)}, f32[400,6400]{1,0:T(8,128)}, f32[1600,1600]{1,0:T(8,128)}) async-done(((f32[400,4800]{1,0:T(8,128)}, f32[400,1600]{1,0:T(8,128)}, f32[400,6400]{1,0:T(8,128)}, f32[1600,1600]{1,0:T(8,128)}), (f32[400,4800]{1,0:T(8,128)}, f32[400,1600]{1,0:T(8,128)}, f32[400,6400]{1,0:T(8,128)}, ...) | async-done | bytes 30720016 | tf_op jit(solution)/shard_map/psum | solution.py:241
  3054.6 7.1 copy.153
  3063.2 9.3 copy.155
  (237 shorter events, 122.6 us)
Async XLA Ops:
  7.2 254.4 %all-gather.6.cloned.1.call-start = ((), (), s32[]{:S(2)}) async-start(), calls=%async_computation.6 | async-start | bytes 3686400 | tf_op jit(solution)/shard_map/all_gather | solution.py:119
  7.2 45.6 %collective-permute-start = (bf16[400,4800]{1,0:T(8,128)(2,1)}, bf16[400,4800]{1,0:T(8,128)(2,1)S(1)}, u32[]{:S(2)}, u32[]{:S(2)}) collective-permute-start(bf16[400,4800]{1,0:T(8,128)(2,1)} %param.22), channel_id=1, source_target_pairs={{0,3},{1,0},{2,1},{3,2},{4,7},{5,4},{6,5},{7,6},{8,11},{9,8},{10,9... | collective-permute-start | bytes 11520008 | tf_op jit(solution)/shard_map/ppermute | solution.py:89
  54.7 44.6 %collective-permute-start.1 = (bf16[400,4800]{1,0:T(8,128)(2,1)S(1)}, bf16[400,4800]{1,0:T(8,128)(2,1)}, u32[]{:S(2)}, u32[]{:S(2)}) collective-permute-start(bf16[400,4800]{1,0:T(8,128)(2,1)S(1)} %collective-permute-done), channel_id=1, source_target_pairs={{0,3},{1,0},{2,1},{3,2},{4,7},{5,4},{6,5},{7,6},{8,11},{9,8},{10,9... | collective-permute-start | bytes 11520008 | tf_op jit(solution)/shard_map/ppermute | solution.py:89
  99.3 67.0 %collective-permute-start.2 = (bf16[400,4800]{1,0:T(8,128)(2,1)}, bf16[400,4800]{1,0:T(8,128)(2,1)}, u32[]{:S(2)}, u32[]{:S(2)}) collective-permute-start(bf16[400,4800]{1,0:T(8,128)(2,1)} %collective-permute-done.1), channel_id=1, source_target_pairs={{0,3},{1,0},{2,1},{3,2},{4,7},{5,4},{6,5},{7,6},{8,11},{9,8},{10,9... | collective-permute-start | bytes 11520008 | tf_op jit(solution)/shard_map/ppermute | solution.py:89
  152.9 30.4 copy-start.28
  152.9 30.4 copy-start.26
  154.2 29.2 copy-start.32
  155.4 4.4 copy-start.39
  155.4 27.9 copy-start.34
  155.4 4.4 copy-start.8
  166.2 4.4 copy-start.6
  179.0 4.4 copy-start.4
  197.0 129.1 %all-gather.8.cloned.1.call-start = ((), (), s32[]{:S(2)}) async-start(), calls=%async_computation.7 | async-start | bytes 3686400 | tf_op jit(solution)/shard_map/all_gather | solution.py:120
  199.9 166.8 %all-gather.10.cloned.1.call-start = ((), (), s32[]{:S(2)}) async-start(), calls=%async_computation.8 | async-start | bytes 6656000 | tf_op jit(solution)/shard_map/all_gather | solution.py:102
  200.6 296.4 %all-gather.12.cloned.1.call-start = ((), (), s32[]{:S(2)}) async-start(), calls=%async_computation.9 | async-start | bytes 25600000 | tf_op jit(solution)/shard_map/all_gather | solution.py:148
  201.2 430.7 %all-gather.14.cloned.1.call-start = ((), (), s32[]{:S(2)}) async-start(), calls=%async_computation.10 | async-start | bytes 26624000 | tf_op jit(solution)/shard_map/all_gather | solution.py:150
  201.8 873.1 %reduce-scatter.7.cloned.1.call-start = ((), (), s32[]{:S(2)}) async-start(), calls=%async_computation.11 | async-start | bytes 7372800 | tf_op jit(solution)/shard_map/reduce_scatter | solution.py:216
  202.6 294.5 %copy-start.30 = (f32[1600]{0:T(1024)}, f32[1600]{0:T(1024)S(1)}, u32[]{:S(2)}) copy-start(f32[1600]{0:T(1024)S(1)} %convert_element_type.113) | copy-start | bytes 19204
  362.0 9.5 copy-start.15
  371.5 285.2 %copy-start.1 = (f32[128,1600]{0,1:T(8,128)}, f32[128,1600]{0,1:T(8,128)S(1)}, u32[]{:S(2)}) copy-start(f32[128,1600]{0,1:T(8,128)S(1)} %get-tuple-element.354) | copy-start | bytes 2457604
  371.7 260.2 %copy-start.17 = (bf16[1,128,1600]{1,2,0:T(8,128)(2,1)S(1)}, bf16[1,128,1600]{1,2,0:T(8,128)(2,1)}, u32[]{:S(2)}) copy-start(bf16[1,128,1600]{1,2,0:T(8,128)(2,1)} %param.33) | copy-start | bytes 1228804
  643.9 12.7 copy-start.10
  643.9 14.0 slice-start
  644.0 14.0 slice-start.1
  661.0 2.8 copy-start.9
  663.6 5.4 copy-start
  805.6 5.4 copy-start
  952.7 247.9 %reduce-scatter.9.cloned.1.call-start = ((), (), s32[]{:S(2)}) async-start(), calls=%async_computation.12 | async-start | bytes 7372800 | tf_op jit(solution)/shard_map/reduce_scatter | solution.py:217
  960.0 328.5 %reduce-scatter.13.cloned.1.call-start = ((), (), s32[]{:S(2)}) async-start(), calls=%async_computation.14 | async-start | bytes 13312000 | tf_op jit(solution)/shard_map/reduce_scatter | solution.py:238
  966.8 235.2 %copy-start.5 = (bf16[1,128,1600]{1,2,0:T(8,128)(2,1)S(1)}, bf16[1,128,1600]{1,2,0:T(8,128)(2,1)}, u32[]{:S(2)}) copy-start(bf16[1,128,1600]{1,2,0:T(8,128)(2,1)} %param.19) | copy-start | bytes 1228804
  966.9 235.2 %copy-start.27 = (f32[1600]{0:T(1024)S(1)}, f32[1600]{0:T(1024)}, u32[]{:S(2)}) copy-start(f32[1600]{0:T(1024)} %copy-done.26) | copy-start | bytes 19204
  966.9 235.2 %copy-start.29 = (f32[1600]{0:T(1024)S(1)}, f32[1600]{0:T(1024)}, u32[]{:S(2)}) copy-start(f32[1600]{0:T(1024)} %copy-done.28) | copy-start | bytes 19204
  966.9 235.2 %copy-start.33 = (f32[128]{0:T(128)S(1)}, f32[128]{0:T(128)}, u32[]{:S(2)}) copy-start(f32[128]{0:T(128)} %copy-done.32) | copy-start | bytes 1540
  966.9 235.2 %copy-start.35 = (f32[128]{0:T(128)S(1)}, f32[128]{0:T(128)}, u32[]{:S(2)}) copy-start(f32[128]{0:T(128)} %copy-done.34) | copy-start | bytes 1540
  966.9 545.9 %reduce-scatter.11.cloned.1.call-start = ((), (), s32[]{:S(2)}) async-start(), calls=%async_computation.13 | async-start | bytes 38912000 | tf_op jit(solution)/shard_map/reduce_scatter | solution.py:236
  1076.1 143.6 %copy-start.22 = (bf16[128,1600]{0,1:T(8,128)(2,1)}, bf16[128,1600]{0,1:T(8,128)(2,1)S(1)}, u32[]{:S(2)}) copy-start(bf16[128,1600]{0,1:T(8,128)(2,1)S(1)} %convert_element_type.124) | copy-start | bytes 1228804
  1202.0 17.7 copy-start.24
  1219.8 588.5 %reduce-scatter.15.cloned.1.call-start = ((), (), s32[]{:S(2)}) async-start(), calls=%async_computation.15 | async-start | bytes 51200000 | tf_op jit(solution)/shard_map/reduce_scatter | solution.py:178
  1238.8 858.7 %reduce-scatter.17.cloned.1.call-start = ((), (), s32[]{:S(2)}) async-start(), calls=%async_computation.16 | async-start | bytes 53248000 | tf_op jit(solution)/shard_map/reduce_scatter | solution.py:180
  1258.7 875.1 %all-reduce.25.cloned.1.call-start = ((), (), s32[]{:S(2)}) async-start(), calls=%async_computation.18 | async-start | bytes 188416
  1259.8 9.9 copy-start.40
  1259.8 11.1 copy-start.14
  1259.8 11.1 copy-start.38
  1272.9 1781.8 %all-reduce.23.cloned.1.call-start = ((), (), s32[]{:S(2)}) async-start(), calls=%async_computation.17 | async-start | bytes 62668800 | tf_op jit(solution)/shard_map/psum | solution.py:241
  3054.6 7.1 copy-start.21
  3061.7 10.8 slice-start.2
  3063.2 9.3 slice-start.3
  3063.2 9.3 slice-start.4
  (17 other events, 25.9 us)
Sparse Core Ops, SparseCore 0:
  197.1 64.4 all-gather.5
  263.7 62.3 all-gather.7
  327.6 39.0 all-gather.9
  368.1 128.8 all-gather.11
  498.4 133.3 all-gather.13
  952.8 122.1 reduce-scatter.6
  1079.2 121.3 reduce-scatter.8
  1203.8 84.6 reduce-scatter.12
  1291.1 221.6 reduce-scatter.10
  1515.2 292.9 reduce-scatter.14
  1810.9 286.6 reduce-scatter.16
  2101.4 32.2 all-reduce.24
  2138.6 915.9 all-reduce.22
